TPU v7x, 32 devices: a whole 2x2x4 slice. The times are simulated.
32 devices in a mesh: lat: 8 (over z, x), lev: 4 (over y, core).
Axes of the slice: x: 2, y: 2, z: 4, core: 2. Of those that a mesh axis runs over, the one named last changes fastest.
Arguments:
- fourier: bfloat16 [1280, 640, 1024], P('lat', None, 'lev'), may hold values from -6 to 6
- legendre: bfloat16 [640, 2, 640, 320], P('lat', None, 'lev'), may hold values from -0.25 to 0.25
- owner: int32 [640], replicated, may hold values from 0 to 7, as said below
Outputs:
- spectral: bfloat16 [640, 2, 320, 1024], P('lat', None, None, 'lev')
Inputs may be any that keep to these rules, and one draw needn't show every extreme that they name: `owner`: each index along lat is named by exactly 80 wavenumbers.
All inputs are finite; a program needn't handle non-finite values.
Results may differ from a plain program's by a relative error of at most 0.0051.
Values may be sent and summed in bfloat16 or wider, within the bound.
A program may use at most 384 MiB of HBM per device.

v0:
```python
import jax
import jax.numpy as jnp
from jax import lax
from jax.sharding import PartitionSpec as P


def slot_waves(owner, slot_count):
    wave_count = owner.shape[0]
    wave_ids = jnp.arange(wave_count, dtype=jnp.int32)
    earlier = (owner[None, :] == owner[:, None]) & (wave_ids[None, :] < wave_ids[:, None])
    ranked = jnp.sum(earlier.astype(jnp.int32), axis=1)
    placed = owner * slot_count + ranked
    matched = placed[None, :] == wave_ids[:, None]
    return jnp.sum(jnp.where(matched, wave_ids[None, :], 0), axis=1)


def block_product(tile_part, source_part):
    return lax.dot_general(
        tile_part, source_part, (((0,), (0,)), ((), ())), preferred_element_type=jnp.float32
    )


def block_zeros(tile_part, source_part):
    return jnp.zeros((tile_part.shape[1], source_part.shape[1]), jnp.float32)


def project_slot(operands):
    table_part, even_rows, odd_rows, counts = operands
    half_rows = table_part.shape[2]
    results = []
    for parity in range(2):
        source = even_rows if parity == 0 else odd_rows
        blocks = []
        for block_low in range(0, half_rows, 128):
            block_high = min(block_low + 128, half_rows)
            tile_part = table_part[parity, :, block_low:block_high]
            blocks.append(
                lax.cond(counts[parity] > block_low, block_product, block_zeros, tile_part, source)
            )
        results.append(jnp.concatenate(blocks, axis=0))
    return jnp.stack(results)


def body(fourier, legendre, owner):
    lat_count = lax.axis_size("lat")
    row_count, wave_count, column_count = fourier.shape
    slot_count = wave_count // lat_count
    north_count = row_count * lat_count // 2
    wave_of = slot_waves(owner, slot_count)
    own_waves = lax.dynamic_slice_in_dim(wave_of, lax.axis_index("lat") * slot_count, slot_count)
    parities = jnp.arange(2, dtype=jnp.int32)
    live_count = (wave_count - own_waves[:, None] - parities[None, :] + 1) // 2
    outgoing = jnp.swapaxes(jnp.take(fourier, wave_of, axis=1), 0, 1)
    arrived = lax.all_to_all(outgoing, "lat", split_axis=0, concat_axis=1, tiled=True)
    upper_rows = arrived[:, :north_count].astype(jnp.float32)
    lower_rows = arrived[:, north_count:].astype(jnp.float32)
    even_part = (upper_rows + lower_rows).astype(jnp.bfloat16)
    odd_part = (upper_rows - lower_rows).astype(jnp.bfloat16)
    half_rows = legendre.shape[3]
    initial = jnp.zeros((slot_count, 2, half_rows, column_count), jnp.float32)
    totals = initial + lax.map(
        project_slot,
        (lax.all_gather(legendre, "lev", axis=2, tiled=True), even_part, odd_part, live_count),
    )
    degree = jnp.arange(half_rows, dtype=jnp.int32)
    kept_mask = degree[None, None, :] < live_count[:, :, None]
    return jnp.where(kept_mask[..., None], totals, 0.0).astype(jnp.bfloat16)


def solution(mesh):
    placed = (P("lat", None, "lev"), P("lat", None, "lev", None), P())
    return jax.shard_map(
        body, mesh=mesh, in_specs=placed, out_specs=P("lat", None, None, "lev"), check_vma=False
    )
```

profile of v0, /device:TPU:0, one launch (start us, length us, event | category | flops | bytes accessed | tf_op | source)
XLA Modules:
  0.0 2179.2 jit_solution(2345935885412572591)
XLA Ops:
  9.9 103.6 %gather_fusion = bf16[640,160,256]{2,0,1:T(8,128)(2,1)} fusion(bf16[160,640,256]{2,1,0:T(8,128)(2,1)} %param.17, s32[1024]{0:T(1024)S(1)} %pad_clamp_fusion), kind=kCustom, calls=%fused_computation | custom fusion | bytes 104860160 | tf_op jit(solution)/shard_map/jit(_take)/gather | solution.py:53
  113.4 34.9 %broadcast_select_fusion = bf16[640,160,256]{2,0,1:T(8,128)(2,1)} fusion(bf16[640,160,256]{2,0,1:T(8,128)(2,1)} %gather_fusion, pred[640]{0:T(1024)(128)(4,1)S(1)} %compare_and_fusion), kind=kLoop, calls=%fused_computation.32 | loop fusion | flops 26214400 | bytes 104858240 | tf_op jit(solution)/shard_map/jit(_take)/select_n | solution.py:53
  148.3 47.6 %copy.12 = bf16[640,160,256]{2,1,0:T(8,128)(2,1)} copy(bf16[640,160,256]{2,0,1:T(8,128)(2,1)} %broadcast_select_fusion) | data formatting | bytes 104857600 | tf_op jit(solution)/shard_map/jit(_take)/select_n | solution.py:53
  195.9 8.8 all-to-all-start
  205.8 1127.9 %all-to-all-done = bf16[640,160,256]{2,1,0:T(8,128)(2,1)} async-done(((bf16[640,160,256]{2,1,0:T(8,128)(2,1)}), bf16[640,160,256]{2,1,0:T(8,128)(2,1)}, u32[]{:S(2)}, u32[]{:S(2)}) %all-to-all-start) | async-done | bytes 52428832 | tf_op jit(solution)/shard_map/all_to_all | solution.py:54
  1333.7 34.9 %copy.13 = bf16[80,8,160,256]{3,2,1,0:T(8,128)(2,1)} copy(bf16[80,8,160,256]{3,2,0,1:T(8,128)(2,1)} %bitcast.19) | data formatting | bytes 104857600 | tf_op jit(solution)/shard_map/all_to_all | solution.py:54
  1368.5 35.3 %fusion.20 = (bf16[80,640,256]{2,1,0:T(8,128)(2,1)}, bf16[80,640,256]{2,1,0:T(8,128)(2,1)}) fusion(bf16[80,1280,256]{2,1,0:T(8,128)(2,1)} %bitcast.81), kind=kLoop, calls=%fused_computation.30 | loop fusion | flops 78643200 | bytes 104857600 | tf_op jit(solution)/shard_map/convert_element_type | solution.py:58
  1403.8 750.2 %while.11 = (s32[]{:T(128)}, bf16[80,2,320,256]{3,2,1,0:T(8,128)(2,1)}, s32[80,2]{0,1:T(2,128)S(1)}, bf16[80,2,640,320]{3,2,1,0:T(8,128)(2,1)}, bf16[80,640,256]...) while((s32[]{:T(128)}, ...), condition=%wide.region_15.16_spmd.clone, body=%wide.region_2.15_spmd.sunk.clone | while | flops 211353600 | bytes 7537453 | solution.py:61
  1405.0 1.3 dynamic-slice_bitcast_fusion.7
  1414.7 1.3 dynamic-slice_bitcast_fusion.7
  1424.3 1.3 dynamic-slice_bitcast_fusion.7
  1434.0 1.3 dynamic-slice_bitcast_fusion.7
  1443.7 1.3 dynamic-slice_bitcast_fusion.7
  1453.4 1.3 dynamic-slice_bitcast_fusion.7
  1463.0 1.3 dynamic-slice_bitcast_fusion.7
  1472.7 1.3 dynamic-slice_bitcast_fusion.7
  1482.4 1.3 dynamic-slice_bitcast_fusion.7
  1492.1 1.3 dynamic-slice_bitcast_fusion.7
  1501.7 1.3 dynamic-slice_bitcast_fusion.7
  1511.4 1.3 dynamic-slice_bitcast_fusion.7
  1521.1 1.3 dynamic-slice_bitcast_fusion.7
  1530.8 1.3 dynamic-slice_bitcast_fusion.7
  1540.5 1.3 dynamic-slice_bitcast_fusion.7
  1550.1 1.3 dynamic-slice_bitcast_fusion.7
  1559.8 1.3 dynamic-slice_bitcast_fusion.7
  1569.5 1.3 dynamic-slice_bitcast_fusion.7
  1579.2 1.3 dynamic-slice_bitcast_fusion.7
  1588.8 1.3 dynamic-slice_bitcast_fusion.7
  1598.5 1.3 dynamic-slice_bitcast_fusion.7
  1608.2 1.3 dynamic-slice_bitcast_fusion.7
  1617.9 1.3 dynamic-slice_bitcast_fusion.7
  1627.6 1.3 dynamic-slice_bitcast_fusion.7
  1637.2 1.3 dynamic-slice_bitcast_fusion.7
  1646.5 1.3 dynamic-slice_bitcast_fusion.7
  1655.7 1.3 dynamic-slice_bitcast_fusion.7
  1665.0 1.3 dynamic-slice_bitcast_fusion.7
  1674.2 1.3 dynamic-slice_bitcast_fusion.7
  1683.5 1.3 dynamic-slice_bitcast_fusion.7
  1692.7 1.3 dynamic-slice_bitcast_fusion.7
  1702.0 1.3 dynamic-slice_bitcast_fusion.7
  1711.2 1.3 dynamic-slice_bitcast_fusion.7
  1720.5 1.3 dynamic-slice_bitcast_fusion.7
  1729.7 1.3 dynamic-slice_bitcast_fusion.7
  1739.0 1.3 dynamic-slice_bitcast_fusion.7
  1757.5 1.3 dynamic-slice_bitcast_fusion.7
  1766.7 1.3 dynamic-slice_bitcast_fusion.7
  1776.0 1.3 dynamic-slice_bitcast_fusion.7
  1813.0 1.3 dynamic-slice_bitcast_fusion.7
  1831.5 1.3 dynamic-slice_bitcast_fusion.7
  1850.0 1.3 dynamic-slice_bitcast_fusion.7
  1868.5 1.3 dynamic-slice_bitcast_fusion.7
  1887.0 1.3 dynamic-slice_bitcast_fusion.7
  1905.5 1.3 dynamic-slice_bitcast_fusion.7
  1951.7 1.3 dynamic-slice_bitcast_fusion.7
  1970.2 1.3 dynamic-slice_bitcast_fusion.7
  1988.7 1.3 dynamic-slice_bitcast_fusion.7
  2007.2 1.3 dynamic-slice_bitcast_fusion.7
  2025.7 1.3 dynamic-slice_bitcast_fusion.7
  2044.2 1.3 dynamic-slice_bitcast_fusion.7
  2081.2 1.3 dynamic-slice_bitcast_fusion.7
  2090.4 1.3 dynamic-slice_bitcast_fusion.7
  2099.7 1.3 dynamic-slice_bitcast_fusion.7
  2145.9 1.3 dynamic-slice_bitcast_fusion.7
  2154.1 18.3 select_convert_fusion
  (1481 shorter events, 433.4 us)
Async XLA Ops:
  6.5 1397.3 %all-gather.2.cloned.1.call-start = ((), (), s32[]{:S(2)}) async-start(), calls=%async_computation.1 | async-start | bytes 98304000 | tf_op jit(solution)/shard_map/all_gather | solution.py:63
  9.3 0.6 copy-start
  195.9 1137.8 %all-to-all-start = ((bf16[640,160,256]{2,1,0:T(8,128)(2,1)}), bf16[640,160,256]{2,1,0:T(8,128)(2,1)}, u32[]{:S(2)}, u32[]{:S(2)}) async-start(bf16[640,160,256]{2,1,0:T(8,128)(2,1)} %copy.12), calls=%async_computation | async-start | bytes 104857600 | tf_op jit(solution)/shard_map/all_to_all | solution.py:54
Sparse Core Ops, SparseCore 0:
  8.9 461.6 all-gather.1
where the time goes:
time: 2200 us; the launch traced here: 2180 us
  waiting for transfers between devices  1130 us (51%)
  local copies, waits for them, and re-layouts  435 us (20%)
  loops' own time  349 us (16%)
  other arithmetic  154 us (7%)
  matrix products  90.2 us (4%)
    all_to_all x1, waiting for transfers between devices, body(): lax.all_to_all(outgoing, 'lat', split_axis=0, concat_axis=1, tiled=True)  1130 us
    another operation x1, loops' own time, body(): lax.map(project_slot, (lax.all_gather(legendre, 'lev', axis=2, tiled=True...  340 us
    squeeze x160, local copies, waits for them, and re-layouts, body(): lax.map(project_slot, (lax.all_gather(legendre, 'lev', axis=2, tiled=True...  194 us
    gather x1, local copies, waits for them, and re-layouts, body(): outgoing = jnp.swapaxes(jnp.take(fourier, wave_of, axis=1), 0, 1)  104 us
    dot_general x368, matrix products, block_product(): lax.dot_general(tile_part, source_part, (((0,), (0,)), ((), ())), preferr...  90.2 us
    dynamic_update_slice x80, other arithmetic, body(): lax.map(project_slot, (lax.all_gather(legendre, 'lev', axis=2, tiled=True...  60.2 us
    slice x80, local copies, waits for them, and re-layouts, project_slot(): counts[parity] > block_low  48 us
    select_n x1, local copies, waits for them, and re-layouts, body(): outgoing = jnp.swapaxes(jnp.take(fourier, wave_of, axis=1), 0, 1)  47.6 us
  transfers between devices with their start and end apart: 2, of which 1 were waited for; matrix products, arithmetic and copies ran while one was open for 12% of the time, Pallas kernels for 0%

commit v1 on v0

v1 whole, which is shorter than its diff:
```python
import functools

import jax
import jax.numpy as jnp
from jax import lax
from jax.experimental import pallas as pl
from jax.experimental.pallas import tpu as pltpu
from jax.sharding import PartitionSpec as P

CHUNKS = 2


def slot_places(owner, slot_count):
    wave_count = owner.shape[0]
    wave_ids = jnp.arange(wave_count, dtype=jnp.int32)
    earlier = (owner[None, :] == owner[:, None]) & (wave_ids[None, :] < wave_ids[:, None])
    ranked = jnp.sum(earlier.astype(jnp.int32), axis=1)
    placed = owner * slot_count + ranked
    return placed[None, :] == wave_ids[:, None]


def project(base, wave_count, waves_ref, rows_ref, table_ref, *rest):
    out_ref = rest[-1]
    half_rows, column_count = out_ref.shape[2:]
    half = rows_ref.shape[0] // 2
    upper = rows_ref[:half, 0].astype(jnp.float32).reshape(-1, column_count)
    lower = rows_ref[half:, 0].astype(jnp.float32).reshape(-1, column_count)
    wave = waves_ref[base + pl.program_id(0)]
    degree = lax.broadcasted_iota(jnp.int32, (half_rows, column_count), 0)
    for parity in range(2):
        part = (upper + lower if parity == 0 else upper - lower).astype(jnp.bfloat16)
        total = lax.dot_general(
            table_ref[0, parity], part, (((0,), (0,)), ((), ())),
            preferred_element_type=jnp.float32,
        )
        live = (wave_count - wave - parity + 1) // 2
        out_ref[0, parity] = jnp.where(degree < live, total, 0.0).astype(out_ref.dtype)


def project_chunk(base, wave_count, own_waves, rows, table, previous):
    groups, chunk_slots, group_rows, column_count = rows.shape
    slot_count, _, north_count, half_rows = table.shape
    in_specs = [
        pl.BlockSpec((groups, 1, group_rows, column_count), lambda s, w: (0, s, 0, 0)),
        pl.BlockSpec((1, 2, north_count, half_rows), lambda s, w: (base + s, 0, 0, 0)),
    ]
    operands = [own_waves, rows, table]
    aliases = {}
    if previous is not None:
        in_specs.append(pl.BlockSpec(memory_space=pl.ANY))
        operands.append(previous)
        aliases = {3: 0}
    return pl.pallas_call(
        functools.partial(project, base, wave_count),
        grid_spec=pltpu.PrefetchScalarGridSpec(
            num_scalar_prefetch=1,
            grid=(chunk_slots,),
            in_specs=in_specs,
            out_specs=pl.BlockSpec(
                (1, 2, half_rows, column_count), lambda s, w: (base + s, 0, 0, 0)
            ),
        ),
        out_shape=jax.ShapeDtypeStruct(
            (slot_count, 2, half_rows, column_count), jnp.bfloat16
        ),
        input_output_aliases=aliases,
        compiler_params=pltpu.CompilerParams(vmem_limit_bytes=32 * 1024 * 1024),
        cost_estimate=pl.CostEstimate(
            flops=4 * chunk_slots * north_count * half_rows * column_count,
            bytes_accessed=2 * rows.size
            + 4 * chunk_slots * half_rows * (north_count + column_count),
            transcendentals=0,
        ),
    )(*operands)


def body(fourier, legendre, owner):
    lat_count = lax.axis_size("lat")
    row_count, wave_count, column_count = fourier.shape
    slot_count = wave_count // lat_count
    matched = slot_places(owner, slot_count)
    wave_ids = jnp.arange(wave_count, dtype=jnp.int32)
    wave_of = jnp.sum(jnp.where(matched, wave_ids[None, :], 0), axis=1)
    own_waves = lax.dynamic_slice_in_dim(wave_of, lax.axis_index("lat") * slot_count, slot_count)
    table = lax.all_gather(legendre, "lev", axis=2, tiled=True)
    picks = matched.astype(jnp.bfloat16).reshape(lat_count, slot_count, wave_count)
    chunks = CHUNKS if slot_count % CHUNKS == 0 else 1
    chunk_slots = slot_count // chunks
    result = None
    for chunk in range(chunks):
        base = chunk * chunk_slots
        pick = picks[:, base : base + chunk_slots].reshape(-1, wave_count)
        outgoing = lax.dot_general(
            pick, fourier, (((1,), (1,)), ((), ())), preferred_element_type=jnp.bfloat16
        )
        arrived = lax.all_to_all(outgoing, "lat", split_axis=0, concat_axis=0, tiled=True)
        arrived = arrived.reshape(lat_count, chunk_slots, row_count, column_count)
        if row_count % 16 != 0:
            arrived = arrived.reshape(2, lat_count // 2, chunk_slots, row_count, column_count)
            arrived = arrived.swapaxes(1, 2).reshape(2, chunk_slots, -1, column_count)
        result = project_chunk(base, wave_count, own_waves, arrived, table, result)
    return result


def solution(mesh):
    placed = (P("lat", None, "lev"), P("lat", None, "lev", None), P())
    return jax.shard_map(
        body, mesh=mesh, in_specs=placed, out_specs=P("lat", None, None, "lev"), check_vma=False
    )
```

time: 2200 us -> 1290 us (0.59); the launches traced: 2180 us -> 1290 us
  local copies, waits for them, and re-layouts: 435 us -> 68.3 us
  loops' own time: 349 us -> 0 us
  other arithmetic: 154 us -> 2.3 us
  waiting for transfers between devices: 1130 us -> 1010 us
  Pallas kernels: 0 us -> 89.9 us
    another operation x481 -> x0, loops' own time: 349 us -> none  [the longest x1 340 us: body(): lax.map(project_slot, (lax.all_gather(legendre, 'lev', axis=2, tiled=True...]
    squeeze x160 -> x0, local copies, waits for them, and re-layouts: 194 us -> none  [body(): lax.map(project_slot, (lax.all_gather(legendre, 'lev', axis=2, tiled=True...]
    all_to_all x1 -> x2, waiting for transfers between devices: 1130 us -> 1010 us  [body(): lax.all_to_all(outgoing, 'lat', split_axis=0, concat_axis=0, tiled=True)]
    gather x1 -> x0, local copies, waits for them, and re-layouts: 104 us -> none  [body(): outgoing = jnp.swapaxes(jnp.take(fourier, wave_of, axis=1), 0, 1)]
    pallas_call x0 -> x2, Pallas kernels: none -> 89.9 us  [project_chunk(): pl.pallas_call(functools.partial(project, base, wave_count), grid_spec=pl...]
    dot_general x0 -> x2, local copies, waits for them, and re-layouts: none -> 68.1 us  [body(): lax.dot_general(pick, fourier, (((1,), (1,)), ((), ())), preferred_elemen...]
    dynamic_update_slice x80 -> x0, other arithmetic: 60.2 us -> none  [body(): lax.map(project_slot, (lax.all_gather(legendre, 'lev', axis=2, tiled=True...]
    convert_element_type x2 -> x0, other arithmetic: 53.6 us -> none  [the longest x1 35.3 us: body(): odd_part = (upper_rows - lower_rows).astype(jnp.bfloat16)]
  transfers between devices with their start and end apart: 2 -> 3, of which waited for: 1 -> 2; matrix products, arithmetic and copies ran while one was open for 12% -> 13% of each run, Pallas kernels for 0% -> 3%
where the time goes in v1:
time: 1290 us
  waiting for transfers between devices  1010 us (78%)
  matrix products  91.5 us (7%)
  Pallas kernels  89.9 us (7%)
  local copies, waits for them, and re-layouts  68.3 us (5%)
  starting transfers between devices  13.9 us (1%)
  between operations  13.4 us (1%)
    all_to_all x2, waiting for transfers between devices, body(): lax.all_to_all(outgoing, 'lat', split_axis=0, concat_axis=0, tiled=True)  1010 us
    dot_general x2, matrix products, body(): lax.dot_general(pick, fourier, (((1,), (1,)), ((), ())), preferred_elemen...  91.5 us
    pallas_call x2, Pallas kernels, project_chunk(): pl.pallas_call(functools.partial(project, base, wave_count), grid_spec=pl...  89.9 us
    dot_general x2, local copies, waits for them, and re-layouts, body(): lax.dot_general(pick, fourier, (((1,), (1,)), ((), ())), preferred_elemen...  68.1 us
  transfers between devices with their start and end apart: 3, of which 2 were waited for; matrix products, arithmetic and copies ran while one was open for 13% of the time, Pallas kernels for 3%

profile of v1, /device:TPU:0, one launch (start us, length us, event | category | flops | bytes accessed | tf_op | source)
XLA Modules:
  0.0 1291.4 jit_solution(289883555846234481)
XLA Ops:
  6.5 0.0 all-gather.2.cloned.1.call-start
  6.5 0.7 all-gather.2.cloned.1.call-update
  7.3 1.1 convert_reduce_fusion
  8.3 0.7 multiply_add_fusion.1
  9.0 0.3 broadcast_compare_fusion
  9.3 0.1 fusion.1
  9.4 50.7 %fusion.3 = bf16[320,160,256]{2,0,1:T(8,128)(2,1)} fusion(pred[320,640,1]{1,0,2:T(8,128)(4,1)S(1)} %bitcast.13, bf16[160,640,256]{2,1,0:T(8,128)(2,1)} %param.3), kind=kOutput, calls=%fused_computation.10 | convolution fusion | flops 16777216000 | bytes 78848000 | tf_op jit(solution)/shard_map/dot_general | solution.py:93
  60.0 34.2 %copy.10 = bf16[320,160,256]{2,1,0:T(8,128)(2,1)} copy(bf16[320,160,256]{2,0,1:T(8,128)(2,1)} %fusion.3) | data formatting | bytes 52428800 | tf_op jit(solution)/shard_map/dot_general | solution.py:93
  94.2 7.2 all-to-all-start.1
  101.5 40.8 %fusion.2 = bf16[320,160,256]{2,0,1:T(8,128)(2,1)} fusion(pred[320,640,1]{1,0,2:T(8,128)(4,1)S(1)} %bitcast.12, bf16[160,640,256]{2,1,0:T(8,128)(2,1)} %param.3), kind=kOutput, calls=%fused_computation.9 | convolution fusion | flops 16777216000 | bytes 78848000 | tf_op jit(solution)/shard_map/dot_general | solution.py:93
  142.3 34.0 %copy.9 = bf16[320,160,256]{2,1,0:T(8,128)(2,1)} copy(bf16[320,160,256]{2,0,1:T(8,128)(2,1)} %fusion.2) | data formatting | bytes 52428800 | tf_op jit(solution)/shard_map/dot_general | solution.py:93
  176.2 492.0 %all-to-all-done.1 = bf16[320,160,256]{2,1,0:T(8,128)(2,1)} async-done(((bf16[320,160,256]{2,1,0:T(8,128)(2,1)}), bf16[320,160,256]{2,1,0:T(8,128)(2,1)}, u32[]{:S(2)}, u32[]{:S(2)}) %all-to-all-start.1) | async-done | bytes 26214432 | tf_op jit(solution)/shard_map/all_to_all | solution.py:96
  668.2 6.7 all-to-all-start
  674.9 0.2 select_reduce_fusion
  675.1 0.1 dynamic_slice.3.waves_ref
  675.2 0.0 all-gather.2.cloned.1.call-done.table_ref
  675.2 44.9 %shard_map.37.rest_0_ = bf16[80,2,320,256]{3,2,1,0:T(8,128)(2,1)} custom-call(s32[80]{0:T(128)S(1)} %dynamic_slice.3.waves_ref, bf16[8,40,160,256]{3,2,1,0:T(8,128)(2,1)} %bitcast.5.rows_ref, bf16[80,2,640,320]{3,2,1,0:T(8,128)(2,1)} %all-gather.2.cloned.1.call-done.table_ref), custom_call_target="tpu_custom_call" | custom-call | flops 8388608000 | bytes 72089600 | tf_op jit(solution)/shard_map/pallas_call | solution.py:53
  720.1 519.5 %all-to-all-done = bf16[320,160,256]{2,1,0:T(8,128)(2,1)} async-done(((bf16[320,160,256]{2,1,0:T(8,128)(2,1)}), bf16[320,160,256]{2,1,0:T(8,128)(2,1)}, u32[]{:S(2)}, u32[]{:S(2)}) %all-to-all-start) | async-done | bytes 26214432 | tf_op jit(solution)/shard_map/all_to_all | solution.py:96
  1239.6 45.0 %shard_map.38 = bf16[80,2,320,256]{3,2,1,0:T(8,128)(2,1)} custom-call(s32[80]{0:T(128)S(1)} %dynamic_slice.3.waves_ref, bf16[8,40,160,256]{3,2,1,0:T(8,128)(2,1)} %bitcast.2.rows_ref, bf16[80,2,640,320]{3,2,1,0:T(8,128)(2,1)} %all-gather.2.cloned.1.call-done.table_ref, bf16[80,2,320,256]{3,2,1,0:T(8,128)(2,1)} %shard_map.37.rest_0_), custom_call_target="tpu_custom_call", output_to_operand_aliasing={{}: (3, {})} | custom-call | flops 8388608000 | bytes 72089600 | tf_op jit(solution)/shard_map/pallas_call | solution.py:53
  (1 shorter events, 0.0 us)
Async XLA Ops:
  6.5 668.7 %all-gather.2.cloned.1.call-start = ((), (), s32[]{:S(2)}) async-start(), calls=%async_computation.2 | async-start | bytes 98304000 | tf_op jit(solution)/shard_map/all_gather | solution.py:85
  94.2 574.0 %all-to-all-start.1 = ((bf16[320,160,256]{2,1,0:T(8,128)(2,1)}), bf16[320,160,256]{2,1,0:T(8,128)(2,1)}, u32[]{:S(2)}, u32[]{:S(2)}) async-start(bf16[320,160,256]{2,1,0:T(8,128)(2,1)} %copy.10), calls=%async_computation.1 | async-start | bytes 52428800 | tf_op jit(solution)/shard_map/all_to_all | solution.py:96
  668.2 571.4 %all-to-all-start = ((bf16[320,160,256]{2,1,0:T(8,128)(2,1)}), bf16[320,160,256]{2,1,0:T(8,128)(2,1)}, u32[]{:S(2)}, u32[]{:S(2)}) async-start(bf16[320,160,256]{2,1,0:T(8,128)(2,1)} %copy.9), calls=%async_computation | async-start | bytes 52428800 | tf_op jit(solution)/shard_map/all_to_all | solution.py:96
Sparse Core Ops, SparseCore 0:
  8.9 461.6 all-gather.1
